TPU v7x, 256 devices: a whole 4x4x8 slice. The times are simulated.
256 devices in a mesh: row: 8 (over z), col: 8 (over y, core), depth: 4 (over x).
Axes of the slice: x: 4, y: 4, z: 8, core: 2. Of those that a mesh axis runs over, the one named last changes fastest.
Arguments:
- a21_leaf: float32 [4, 4096, 2048], P('depth', 'row', 'col'), may hold values from -1.2 to 1.2
- a12_leaf: float32 [4, 2048, 4096], P('depth', 'row', 'col'), may hold values from -1.2 to 1.2
- uinv_leaf: float32 [4, 2048, 2048], P('depth', None, 'col'), may hold values from -0.2 to 1.5, as said below
- linv_leaf: float32 [4, 2048, 2048], P('depth', 'row'), may hold values from -0.2 to 1.5, as said below
- live: int32 [4], P('depth'), may hold values from 16 to 32
- row_map: int32 [4, 32], P('depth', 'row'), may hold values from 0 to 63, as said below
- col_map: int32 [4, 32], P('depth', 'col'), may hold values from 0 to 63, as said below
- a22_anc: float32 [8192, 8192], P(('row', 'depth'), 'col'), may hold values from -6 to 6
- a21_anc: float32 [8192, 2048], P(('row', 'depth'), 'col'), may hold values from -1.2 to 1.2
- a12_anc: float32 [2048, 8192], P(('row', 'depth'), 'col'), may hold values from -1.2 to 1.2
- uinv_anc: float32 [2048, 2048], P(None, 'col'), may hold values from -0.2 to 1.5, as said below
- linv_anc: float32 [2048, 2048], P(('row', 'depth')), may hold values from -0.2 to 1.5, as said below
Outputs:
- leaf_lower: float32 [4, 4096, 2048], P('depth', 'row', 'col')
- leaf_upper: float32 [4, 2048, 4096], P('depth', 'row', 'col')
- anc_lower: float32 [8192, 2048], P(('row', 'depth'), 'col')
- anc_upper: float32 [2048, 8192], P(('row', 'depth'), 'col')
- anc_schur: float32 [8192, 8192], P(('row', 'depth'), 'col')
Inputs may be any that keep to these rules, and one draw needn't show every extreme that they name: `uinv_leaf`: upper triangular: zero below the diagonal, diagonal between 0.5 and 1.5. `linv_leaf`: lower triangular: zero above the diagonal, diagonal between 0.5 and 1.5. `uinv_anc`: upper triangular: zero below the diagonal, diagonal between 0.5 and 1.5. `linv_anc`: lower triangular: zero above the diagonal, diagonal between 0.5 and 1.5. `row_map`: within one replica the entries are distinct. Leaf block row i lies in the k-th of 8 equal ranges of leaf block rows, and its target lies in the k-th of 8 equal ranges of the 64 ancestor block rows. `col_map`: within one replica the entries are distinct. Leaf block column j lies in the k-th of 8 equal ranges of leaf block columns, and its target lies in the k-th of 8 equal ranges of the 64 ancestor block columns.
All inputs are finite; a program needn't handle non-finite values.
Results may differ from a plain program's by a relative error of at most 0.0001.
Values sent between devices are 32-bit elements; how exact they have to be, the bound alone decides.
No kernel may reach another device: no remote copies, remote signals or barrier semaphores. Data moves between devices by JAX's collectives and lax.ppermute only.
A program may use at most 128 MiB of HBM per device.

v0:
```python
import math
import jax
import jax.numpy as jnp
from jax import lax
from jax.sharding import PartitionSpec as P

NB = 128


def in_one_piece(arrays, axis, split_dim, concat_dim, along):
    widths = [math.prod(a.shape[along:]) for a in arrays]
    both = jnp.concatenate(
        [a.reshape(*a.shape[:along], w) for a, w in zip(arrays, widths)], axis=along
    )
    out = lax.all_to_all(both, axis, split_axis=split_dim, concat_axis=concat_dim, tiled=True)
    tiles = jnp.split(out, [sum(widths[:k]) for k in range(1, len(widths))], axis=along)
    return tuple((b.reshape(*out.shape[:along], *a.shape[along:]) for a, b in zip(arrays, tiles)))


def sent_to_all(shard, axis):
    copies = jnp.broadcast_to(shard, (lax.axis_size(axis), *shard.shape))
    return lax.all_to_all(copies, axis, split_axis=0, concat_axis=0, tiled=True)


def in_order(tiles, dim):
    lengths = list(tiles.shape[1:])
    lengths[dim] *= tiles.shape[0]
    return jnp.moveaxis(tiles, 0, dim).reshape(lengths)


def collect(shard, axis, dim):
    tiles = sent_to_all(shard, axis)
    return in_order(tiles, dim)


def gather_axes(shard, axes, dim):
    out = shard
    for number in range(len(axes) - 1, -1, -1):
        out = lax.all_gather(out, axes[number], axis=dim, tiled=True)
    return out


def product(left, right):
    return jnp.dot(left, right, precision=lax.Precision.HIGHEST, preferred_element_type=jnp.float32)


def combine_depth(schur, row_map, col_map, a22_anc):
    block_size = NB
    rows_here = schur.shape[0]
    cols_here = schur.shape[1]
    leaf_rows = rows_here // block_size
    leaf_cols = cols_here // block_size
    anc_rows = a22_anc.shape[0]
    replicas = lax.axis_size("depth")
    anc_row_blocks = anc_rows * replicas // block_size
    anc_col_blocks = a22_anc.shape[1] // block_size
    row_local = row_map[0] - lax.axis_index("row") * anc_row_blocks
    col_local = col_map[0] - lax.axis_index("col") * anc_col_blocks
    owner_blocks = anc_rows // block_size
    slots = min(leaf_rows, owner_blocks)
    owner = row_local // owner_blocks
    earlier = lax.iota(jnp.int32, leaf_rows)[:, None] > lax.iota(jnp.int32, leaf_rows)[None, :]
    same = owner[:, None] == owner[None, :]
    rank = jnp.sum((earlier & same).astype(jnp.int32), axis=1)
    select = (
        (owner[:, None, None] == lax.iota(jnp.int32, replicas)[None, :, None])
        & (rank[:, None, None] == lax.iota(jnp.int32, slots)[None, None, :])
    ).astype(jnp.float32)
    leaf_blocks = schur.reshape(leaf_rows, block_size, cols_here)
    packed = jnp.einsum("iqs,ixc->qsxc", select, leaf_blocks, precision=lax.Precision.HIGHEST)
    packed = packed.reshape(replicas, slots * block_size, cols_here)
    target = (row_local - owner * owner_blocks + 1).astype(jnp.float32)
    tags = jnp.einsum("iqs,i->qs", select, target, precision=lax.Precision.HIGHEST) - 1.0
    col_tags = jnp.broadcast_to(col_local.astype(jnp.float32)[None, :], (replicas, leaf_cols))
    got_rows, got_tags, got_cols = in_one_piece((packed, tags, col_tags), "depth", 0, 0, 1)
    slot_pick = (
        got_tags[:, :, None] == lax.iota(jnp.int32, owner_blocks).astype(jnp.float32)[None, None, :]
    ).astype(jnp.float32)
    column_pick = (
        got_cols[:, :, None]
        == lax.iota(jnp.int32, anc_col_blocks).astype(jnp.float32)[None, None, :]
    ).astype(jnp.float32)
    pieces = got_rows.reshape(replicas, slots, block_size, leaf_cols, block_size)
    sectioned = jnp.einsum("psa,psxjy->paxjy", slot_pick, pieces, precision=lax.Precision.HIGHEST)
    placed = jnp.einsum("paxjy,pjb->axby", sectioned, column_pick, precision=lax.Precision.HIGHEST)
    return placed.reshape(anc_rows, anc_col_blocks * block_size)


def anc_panels(a21_anc, a12_anc, uinv_anc, linv_anc):
    factor = uinv_anc
    anc_lower = product(collect(a21_anc, "col", 1), factor)
    lower_whole = collect(anc_lower, "col", 1)
    factor = linv_anc
    anc_upper = product(factor, lax.all_gather(a12_anc, ("row", "depth"), axis=0, tiled=True))
    return (anc_lower, lower_whole, anc_upper)


def shards(
    a21_leaf,
    a12_leaf,
    uinv_leaf,
    linv_leaf,
    live,
    row_map,
    col_map,
    a22_anc,
    a21_anc,
    a12_anc,
    uinv_anc,
    linv_anc,
):
    block_size = NB
    panel_left = a21_leaf[0]
    panel_top = a12_leaf[0]
    upper_inverse = uinv_leaf[0]
    lower_inverse = linv_leaf[0]
    rows_here = panel_left.shape[0]
    cols_here = panel_top.shape[1]
    live_rows = live[0] * block_size
    row_pos = lax.axis_index("row") * rows_here + lax.iota(jnp.int32, rows_here)
    col_pos = lax.axis_index("col") * cols_here + lax.iota(jnp.int32, cols_here)
    row_keep = (row_pos < live_rows).astype(jnp.float32)
    col_keep = (col_pos < live_rows).astype(jnp.float32)
    factor = upper_inverse
    lower_part = product(lax.all_gather(panel_left, "col", axis=1, tiled=True), factor)
    leaf_lower = lower_part * row_keep[:, None]
    factor = lower_inverse
    upper_part = product(factor, lax.all_gather(panel_top, "row", axis=0, tiled=True))
    leaf_upper = upper_part * col_keep[None, :]
    upper_whole = lax.all_gather(leaf_upper, "row", axis=0, tiled=True)
    factor = upper_whole
    schur = jnp.zeros((rows_here, cols_here), jnp.float32) - product(
        lax.all_gather(leaf_lower, "col", axis=1, tiled=True), factor
    )
    own_update = combine_depth(schur, row_map, col_map, a22_anc)
    anc_lower, lower_whole, anc_upper = anc_panels(a21_anc, a12_anc, uinv_anc, linv_anc)
    factor = lower_whole
    anc_schur = a22_anc + own_update - product(factor, gather_axes(anc_upper, ("row", "depth"), 0))
    return (leaf_lower[None], leaf_upper[None], anc_lower, anc_upper, anc_schur)


def solution(mesh):
    in_specs = (
        P("depth", "row", "col"),
        P("depth", "row", "col"),
        P("depth", None, "col"),
        P("depth", "row", None),
        P("depth"),
        P("depth", "row"),
        P("depth", "col"),
        P(("row", "depth"), "col"),
        P(("row", "depth"), "col"),
        P(("row", "depth"), "col"),
        P(None, "col"),
        P(("row", "depth"), None),
    )
    out_specs = (
        P("depth", "row", "col"),
        P("depth", "row", "col"),
        P(("row", "depth"), "col"),
        P(("row", "depth"), "col"),
        P(("row", "depth"), "col"),
    )
    return jax.shard_map(shards, mesh=mesh, in_specs=in_specs, out_specs=out_specs, check_vma=False)
```

profile of v0, /device:TPU:1, one launch (start us, length us, event | category | flops | bytes accessed | tf_op | source)
XLA Modules:
  0.0 436.7 jit_solution(4254180319421357973)
XLA Ops:
  7.2 0.0 copy-start
  7.2 0.0 all-gather.20.cloned.1.call-start
  7.2 0.7 all-gather.20.cloned.1.call-update
  7.9 0.0 all-gather.22.cloned.1.call-start
  8.0 0.7 all-gather.22.cloned.1.call-update
  8.7 0.0 all-gather.10.cloned.1.call-start
  8.7 0.7 all-gather.10.cloned.1.call-update
  9.4 0.0 all-gather.12.cloned.1.call-start
  10.1 38.6 %all-gather.20.cloned.1.call-done = f32[1,512,2048]{2,1,0:T(8,128)} async-done(((f32[1,512,256]{2,1,0:T(8,128)}), f32[1,512,2048]{2,1,0:T(8,128)}) %all-gather.20.cloned.1.call-update) | async-done | bytes 4194320 | tf_op jit(solution)/shard_map/all_gather | solution.py:125
  48.7 0.0 copy-done
  48.7 6.4 %fusion.10 = f32[512,256]{1,0:T(8,128)} fusion(f32[1,2048,256]{2,1,0:T(8,128)S(1)} %copy-done, f32[1,512,2048]{2,1,0:T(8,128)} %all-gather.20.cloned.1.call-done, f32[512]{0:T(512)S(1)} %fusion.32), kind=kOutput, calls=%fused_computation.13 | convolution fusion | flops 3221356544 | bytes 6817792 | tf_op jit(solution)/shard_map/dot_general | solution.py:44
  55.1 0.0 all-gather.12.cloned.1.call-update
  55.1 0.0 all-gather.14.cloned.1.call-start
  55.2 0.0 copy-start.4
  55.2 49.4 %all-gather.22.cloned.1.call-done = f32[1,2048,512]{2,1,0:T(8,128)} async-done(((f32[1,256,512]{2,1,0:T(8,128)}), f32[1,2048,512]{2,1,0:T(8,128)}) %all-gather.22.cloned.1.call-update) | async-done | bytes 4194320 | tf_op jit(solution)/shard_map/all_gather | solution.py:128
  104.6 7.3 %fusion.15 = f32[256,512]{1,0:T(8,128)} fusion(f32[1,2048,512]{2,1,0:T(8,128)} %all-gather.22.cloned.1.call-done, f32[1,256,2048]{2,1,0:T(8,128)} %param.15, f32[512]{0:T(512)S(1)} %fusion.33), kind=kOutput, calls=%fused_computation.14 | convolution fusion | flops 3221356544 | bytes 6817792 | tf_op jit(solution)/shard_map/dot_general | solution.py:44
  111.9 0.0 all-gather.14.cloned.1.call-update
  112.0 0.0 copy-done.4
  112.0 0.1 copy.29
  112.1 1.5 broadcast_in_dim.16
  113.6 0.0 copy-start.5
  113.6 5.3 %all-to-all-start = ((f32[8,256,256]{1,2,0:T(8,128)}), f32[8,256,256]{1,2,0:T(8,128)S(1)}, u32[]{:S(2)}, u32[]{:S(2)}) async-start(f32[8,256,256]{1,2,0:T(8,128)} %broadcast_in_dim.16), calls=%async_computation | async-start | bytes 4194304 | tf_op jit(solution)/shard_map/all_to_all | solution.py:22
  118.9 0.0 all-gather.16.cloned.1.call-start
  118.9 0.0 copy-done.5
  118.9 0.1 convert_reduce_fusion
  119.0 84.1 %all-gather.10.cloned.1.call-done = f32[2048,1024]{1,0:T(8,128)} async-done(((f32[64,1024]{1,0:T(8,128)}), f32[2048,1024]{1,0:T(8,128)}) %all-gather.10.cloned.1.call-update) | async-done | bytes 8388624 | tf_op jit(solution)/shard_map/all_gather | solution.py:94
  203.1 0.0 copy-done.3
  203.1 8.2 %fusion.51 = f32[64,1024]{1,0:T(8,128)} fusion(f32[64,2048]{1,0:T(8,128)S(1)} %copy-done.3, f32[2048,1024]{1,0:T(8,128)} %all-gather.10.cloned.1.call-done), kind=kOutput, calls=%fused_computation.69 | convolution fusion | flops 1610612736 | bytes 9175040 | tf_op jit(solution)/shard_map/dot_general | solution.py:44
  211.3 0.0 all-gather.16.cloned.1.call-update
  211.4 0.2 all-gather.18.cloned.1.call-start
  211.6 0.1 fusion.27
  211.7 0.1 copy.37
  211.8 0.0 copy-done.6
  211.8 0.1 bitcast_add_fusion.1
  211.9 26.4 %all-gather.12.cloned.1.call-done = f32[512,2048]{1,0:T(8,128)} async-done(((f32[512,256]{1,0:T(8,128)}), f32[512,2048]{1,0:T(8,128)}) %all-gather.12.cloned.1.call-update) | async-done | bytes 4194320 | tf_op jit(solution)/shard_map/all_gather | solution.py:133
  238.3 56.4 %all-gather.14.cloned.1.call-done = f32[2048,512]{1,0:T(8,128)} async-done(((f32[256,512]{1,0:T(8,128)}), f32[2048,512]{1,0:T(8,128)}) %all-gather.14.cloned.1.call-update) | async-done | bytes 4194320 | tf_op jit(solution)/shard_map/all_gather | solution.py:130
  294.7 9.4 %convolution_subtract_fusion = f32[512,512]{1,0:T(8,128)S(1)} fusion(f32[512,2048]{1,0:T(8,128)} %all-gather.12.cloned.1.call-done, f32[2048,512]{1,0:T(8,128)} %all-gather.14.cloned.1.call-done), kind=kOutput, calls=%fused_computation.11 | convolution fusion | flops 6442713088 | bytes 9437184 | tf_op jit(solution)/shard_map/dot_general | solution.py:44
  304.0 3.6 fusion.20
  307.6 12.7 %all-gather.16.cloned.1.call-done = f32[256,1024]{1,0:T(8,128)} async-done(((f32[64,1024]{1,0:T(8,128)}), f32[256,1024]{1,0:T(8,128)}) %all-gather.16.cloned.1.call-update) | async-done | bytes 1048592 | tf_op jit(solution)/shard_map/all_gather | solution.py:39
  320.3 0.0 all-gather.18.cloned.1.call-update
  320.3 3.1 constant_dynamic-update-slice_fusion
  323.4 1.3 dynamic-update-slice.1
  324.7 1.4 dynamic-update-slice.2
  326.0 4.8 %copy.31 = f32[4,1,131078]{2,1,0:T(1,128)} copy(f32[4,1,131078]{2,0,1:T(4,128)} %bitcast.99) | data formatting | bytes 4194496 | tf_op jit(solution)/shard_map/all_to_all | solution.py:15
  330.9 0.0 all-to-all-done
  330.9 4.5 %all-to-all-start.1 = ((f32[4,1,131078]{2,1,0:T(1,128)}), f32[4,1,131078]{2,1,0:T(1,128)}, u32[]{:S(2)}, u32[]{:S(2)}) async-start(f32[4,1,131078]{2,1,0:T(1,128)} %copy.31), calls=%async_computation.1 | async-start | bytes 4198400 | tf_op jit(solution)/shard_map/all_to_all | solution.py:15
  335.4 5.3 %fusion.50 = f32[256,256]{1,0:T(8,128)S(1)} fusion(f32[256,2048]{0,1:T(8,128)S(1)} %bitcast.100, f32[2048,256]{1,0:T(8,128)} %param.22), kind=kOutput, calls=%fused_computation.68 | convolution fusion | flops 1610612736 | bytes 4456448 | tf_op jit(solution)/shard_map/dot_general | solution.py:44
  340.7 0.0 copy-start.2
  340.7 0.1 copy.35
  340.8 18.3 %all-to-all-done.1 = f32[4,1,131078]{2,1,0:T(1,128)} async-done(((f32[4,1,131078]{2,1,0:T(1,128)}), f32[4,1,131078]{2,1,0:T(1,128)}, u32[]{:S(2)}, u32[]{:S(2)}) %all-to-all-start.1) | async-done | bytes 2097280 | tf_op jit(solution)/shard_map/all_to_all | solution.py:15
  359.1 1.5 broadcast_in_dim.20
  360.6 0.0 copy-done.2
  360.6 7.9 %all-to-all-start.2 = ((f32[8,256,256]{1,2,0:T(8,128)}), f32[8,256,256]{1,2,0:T(8,128)}, u32[]{:S(2)}, u32[]{:S(2)}) async-start(f32[8,256,256]{1,2,0:T(8,128)} %broadcast_in_dim.20), calls=%async_computation.2 | async-start | bytes 4194304 | tf_op jit(solution)/shard_map/all_to_all | solution.py:22
  368.5 2.6 copy.53
  371.2 1.5 split.14
  372.7 0.1 split.12
  372.8 3.4 reshape_reshape.7
  376.2 0.1 copy.32
  376.2 4.8 %fusion.8 = f32[4,2,128,4,128]{4,1,3,2,0:T(2,128)S(1)} fusion(f32[4,2,128,4,128]{4,3,2,1,0:T(4,128)S(1)} %reshape_reshape.7, f32[4,2]{1,0:T(4,128)S(1)} %split.13, f32[2]{0:T(128)S(1)} %iota_convert_fusion), kind=kOutput, calls=%fused_computation.9 | convolution fusion | flops 12582928 | bytes 4194344 | tf_op jit(solution)/shard_map/psa,psxjy->paxjy/dot_general | solution.py:84
  381.0 3.2 fusion.6
  384.3 10.6 %all-to-all-done.2 = f32[8,256,256]{1,2,0:T(8,128)} async-done(((f32[8,256,256]{1,2,0:T(8,128)}), f32[8,256,256]{1,2,0:T(8,128)}, u32[]{:S(2)}, u32[]{:S(2)}) %all-to-all-start.2) | async-done | bytes 2097184 | tf_op jit(solution)/shard_map/all_to_all | solution.py:22
  394.8 23.6 %all-gather.18.cloned.1.call-done = f32[2048,1024]{1,0:T(8,128)} async-done(((f32[256,1024]{1,0:T(8,128)}), f32[2048,1024]{1,0:T(8,128)}) %all-gather.18.cloned.1.call-update) | async-done | bytes 8388624 | tf_op jit(solution)/shard_map/all_gather | solution.py:39
  418.5 11.4 %convolution_subtract_fusion.1 = f32[256,1024]{1,0:T(8,128)} fusion(f32[256,2048]{0,1:T(8,128)} %bitcast.28, f32[2048,1024]{1,0:T(8,128)} %all-gather.18.cloned.1.call-done, f32[256,1024]{1,0:T(8,128)} %param.19, f32[32,8,8,128]{3,2,1,0:T(8,128)S(1)} %bitcast.103), kind=kOutput, calls=%fused_computation.12 | convolution fusion | flops 6442975232 | bytes 13631488 | tf_op jit(solution)/shard_map/dot_general | solution.py:44
  429.9 0.0 copy-done.1
  (14 shorter events, 0.1 us)
Async XLA Ops:
  7.2 41.5 %copy-start = (f32[1,2048,256]{2,1,0:T(8,128)S(1)}, f32[1,2048,256]{2,1,0:T(8,128)}, u32[]{:S(2)}) copy-start(f32[1,2048,256]{2,1,0:T(8,128)} %param.14) | copy-start | bytes 6291460
  7.2 41.5 %all-gather.20.cloned.1.call-start = ((), (), s32[]{:S(2)}) async-start(), calls=%async_computation.8 | async-start | bytes 4718592 | tf_op jit(solution)/shard_map/all_gather | solution.py:125
  7.9 96.7 %all-gather.22.cloned.1.call-start = ((), (), s32[]{:S(2)}) async-start(), calls=%async_computation.9 | async-start | bytes 4718592 | tf_op jit(solution)/shard_map/all_gather | solution.py:128
  8.7 194.5 %all-gather.10.cloned.1.call-start = ((), (), s32[]{:S(2)}) async-start(), calls=%async_computation.3 | async-start | bytes 8650752 | tf_op jit(solution)/shard_map/all_gather | solution.py:94
  9.4 228.9 %all-gather.12.cloned.1.call-start = ((), (), s32[]{:S(2)}) async-start(), calls=%async_computation.4 | async-start | bytes 4718592 | tf_op jit(solution)/shard_map/all_gather | solution.py:133
  55.1 239.5 %all-gather.14.cloned.1.call-start = ((), (), s32[]{:S(2)}) async-start(), calls=%async_computation.5 | async-start | bytes 4718592 | tf_op jit(solution)/shard_map/all_gather | solution.py:130
  55.2 56.8 %copy-start.4 = (f32[256,256]{1,0:T(8,128)S(1)}, f32[256,256]{1,0:T(8,128)}, u32[]{:S(2)}) copy-start(f32[256,256]{1,0:T(8,128)} %param.20) | copy-start | bytes 786436
  113.6 5.3 %copy-start.5 = (s32[1,4]{1,0:T(1,128)S(1)}, s32[1,4]{1,0:T(1,128)}, u32[]{:S(2)}) copy-start(s32[1,4]{1,0:T(1,128)} %param.17) | copy-start | bytes 52
  113.6 89.5 %copy-start.3 = (f32[64,2048]{1,0:T(8,128)S(1)}, f32[64,2048]{1,0:T(8,128)}, u32[]{:S(2)}) copy-start(f32[64,2048]{1,0:T(8,128)} %param.23) | copy-start | bytes 1572868
  113.6 217.2 %all-to-all-start = ((f32[8,256,256]{1,2,0:T(8,128)}), f32[8,256,256]{1,2,0:T(8,128)S(1)}, u32[]{:S(2)}, u32[]{:S(2)}) async-start(f32[8,256,256]{1,2,0:T(8,128)} %broadcast_in_dim.16), calls=%async_computation | async-start | bytes 4194304 | tf_op jit(solution)/shard_map/all_to_all | solution.py:22
  118.9 201.4 %all-gather.16.cloned.1.call-start = ((), (), s32[]{:S(2)}) async-start(), calls=%async_computation.6 | async-start | bytes 1310720 | tf_op jit(solution)/shard_map/all_gather | solution.py:39
  119.0 92.8 %copy-start.6 = (s32[1,4]{1,0:T(1,128)S(1)}, s32[1,4]{1,0:T(1,128)}, u32[]{:S(2)}) copy-start(s32[1,4]{1,0:T(1,128)} %param.18) | copy-start | bytes 52
  211.4 207.1 %all-gather.18.cloned.1.call-start = ((), (), s32[]{:S(2)}) async-start(), calls=%async_computation.7 | async-start | bytes 9437184 | tf_op jit(solution)/shard_map/all_gather | solution.py:39
  330.9 28.3 %all-to-all-start.1 = ((f32[4,1,131078]{2,1,0:T(1,128)}), f32[4,1,131078]{2,1,0:T(1,128)}, u32[]{:S(2)}, u32[]{:S(2)}) async-start(f32[4,1,131078]{2,1,0:T(1,128)} %copy.31), calls=%async_computation.1 | async-start | bytes 4198400 | tf_op jit(solution)/shard_map/all_to_all | solution.py:15
  340.7 20.0 %copy-start.2 = (f32[256,256]{1,0:T(8,128)}, f32[256,256]{1,0:T(8,128)S(1)}, u32[]{:S(2)}) copy-start(f32[256,256]{1,0:T(8,128)S(1)} %fusion.50) | copy-start | bytes 786436
  360.6 34.2 %all-to-all-start.2 = ((f32[8,256,256]{1,2,0:T(8,128)}), f32[8,256,256]{1,2,0:T(8,128)}, u32[]{:S(2)}, u32[]{:S(2)}) async-start(f32[8,256,256]{1,2,0:T(8,128)} %broadcast_in_dim.20), calls=%async_computation.2 | async-start | bytes 4194304 | tf_op jit(solution)/shard_map/all_to_all | solution.py:22
  418.5 11.4 %copy-start.1 = (f32[1,2048,256]{2,1,0:T(8,128)S(1)}, f32[1,2048,256]{2,1,0:T(8,128)}, u32[]{:S(2)}) copy-start(f32[1,2048,256]{2,1,0:T(8,128)} %param.14) | copy-start | bytes 6291460
Sparse Core Ops, SparseCore 0:
  9.8 38.8 all-gather.19
  50.5 54.1 all-gather.21
  107.2 95.8 all-gather.9
  205.4 32.8 all-gather.11
  240.5 54.1 all-gather.13
  296.9 23.3 all-gather.15
  322.0 96.3 all-gather.17
where the time goes:
time: 437 us
  waiting for transfers between devices  322 us (74%)
  matrix products  59.7 us (14%)
  local copies, waits for them, and re-layouts  21.7 us (5%)
  starting transfers between devices  18.1 us (4%)
  between operations  14.9 us (3%)
    all_gather x1, waiting for transfers between devices, anc_panels(): lax.all_gather(a12_anc, ('row', 'depth'), axis=0, tiled=True)  84.1 us
    all_gather x1, waiting for transfers between devices, shards(): upper_whole = lax.all_gather(leaf_upper, 'row', axis=0, tiled=True)  56.4 us
    all_gather x1, waiting for transfers between devices, shards(): lax.all_gather(panel_top, 'row', axis=0, tiled=True)  49.4 us
    dot_general x6, matrix products, product(): jnp.dot(left, right, precision=lax.Precision.HIGHEST, preferred_element_t...  48 us
    all_gather x1, waiting for transfers between devices, shards(): lax.all_gather(panel_left, 'col', axis=1, tiled=True)  38.6 us
    all_gather x2, waiting for transfers between devices, gather_axes(): out = lax.all_gather(out, axes[number], axis=dim, tiled=True)  36.3 us
    all_gather x1, waiting for transfers between devices, shards(): lax.all_gather(leaf_lower, 'col', axis=1, tiled=True)  26.4 us
    all_to_all x1, waiting for transfers between devices, in_one_piece(): lax.all_to_all(both, axis, split_axis=split_dim, concat_axis=concat_dim,...  18.3 us
  transfers between devices with their start and end apart: 10, of which 9 were waited for; matrix products, arithmetic and copies ran while one was open for 16% of the time, Pallas kernels for 0%

commit v1 on v0

--- a/solution.py
+++ b/solution.py
@@ -127,7 +127,9 @@
     factor = lower_inverse
     upper_part = product(factor, lax.all_gather(panel_top, "row", axis=0, tiled=True))
     leaf_upper = upper_part * col_keep[None, :]
-    upper_whole = lax.all_gather(leaf_upper, "row", axis=0, tiled=True)
+    upper_whole = jnp.concatenate(
+        lax.all_to_all(jnp.stack([leaf_upper] * lax.axis_size("row")), "row", 0, 0), axis=0
+    )
     factor = upper_whole
     schur = jnp.zeros((rows_here, cols_here), jnp.float32) - product(
         lax.all_gather(leaf_lower, "col", axis=1, tiled=True), factor

time: 437 us -> 459 us (1.050)
  waiting for transfers between devices: 322 us -> 338 us
    all_gather x1, waiting for transfers between devices: 84.1 us -> 144 us  [anc_panels(): lax.all_gather(a12_anc, ('row', 'depth'), axis=0, tiled=True)]
    all_gather x1 -> x0, waiting for transfers between devices: 56.4 us -> none  [shards(): upper_whole = lax.all_gather(leaf_upper, 'row', axis=0, tiled=True)]
    all_gather x1, waiting for transfers between devices: 26.4 us -> 38.4 us  [shards(): lax.all_gather(leaf_lower, 'col', axis=1, tiled=True)]
    all_to_all x0 -> x1, starting transfers between devices: none -> 4.73 us  [shards(): lax.all_to_all(jnp.stack([leaf_upper] * lax.axis_size('row')), 'row', 0, 0)]
  transfers between devices with their start and end apart: 10 -> 10, of which waited for: 9 -> 8; matrix products, arithmetic and copies ran while one was open for 16% -> 16% of each run, Pallas kernels for 0% -> 0%
where the time goes in v1:
time: 459 us
  waiting for transfers between devices  338 us (74%)
  matrix products  58.6 us (13%)
  local copies, waits for them, and re-layouts  24.3 us (5%)
  starting transfers between devices  22.2 us (5%)
  between operations  15 us (3%)
    all_gather x1, waiting for transfers between devices, anc_panels(): lax.all_gather(a12_anc, ('row', 'depth'), axis=0, tiled=True)  144 us
    all_gather x1, waiting for transfers between devices, shards(): lax.all_gather(panel_top, 'row', axis=0, tiled=True)  49.5 us
    dot_general x6, matrix products, product(): jnp.dot(left, right, precision=lax.Precision.HIGHEST, preferred_element_t...  46.9 us
    all_gather x1, waiting for transfers between devices, shards(): lax.all_gather(panel_left, 'col', axis=1, tiled=True)  38.6 us
    all_gather x1, waiting for transfers between devices, shards(): lax.all_gather(leaf_lower, 'col', axis=1, tiled=True)  38.4 us
    all_gather x2, waiting for transfers between devices, gather_axes(): out = lax.all_gather(out, axes[number], axis=dim, tiled=True)  37.4 us
    all_to_all x1, waiting for transfers between devices, in_one_piece(): lax.all_to_all(both, axis, split_axis=split_dim, concat_axis=concat_dim,...  18.3 us
    all_to_all x2, starting transfers between devices, sent_to_all(): return lax.all_to_all(copies, axis, split_axis=0, concat_axis=0, tiled=True)  12.7 us
  transfers between devices with their start and end apart: 10, of which 8 were waited for; matrix products, arithmetic and copies ran while one was open for 16% of the time, Pallas kernels for 0%

profile of v1, /device:TPU:1, one launch (start us, length us, event | category | flops | bytes accessed | tf_op | source)
XLA Modules:
  0.0 458.5 jit_solution(12591166249709123237)
XLA Ops:
  7.2 0.0 copy-start
  7.2 0.0 all-gather.17.cloned.1.call-start
  7.2 0.7 all-gather.17.cloned.1.call-update
  7.9 0.0 all-gather.19.cloned.1.call-start
  8.0 0.7 all-gather.19.cloned.1.call-update
  8.7 0.0 all-gather.9.cloned.1.call-start
  8.7 0.7 all-gather.9.cloned.1.call-update
  9.4 0.0 all-gather.11.cloned.1.call-start
  10.1 38.6 %all-gather.17.cloned.1.call-done = f32[1,512,2048]{2,1,0:T(8,128)} async-done(((f32[1,512,256]{2,1,0:T(8,128)}), f32[1,512,2048]{2,1,0:T(8,128)}) %all-gather.17.cloned.1.call-update) | async-done | bytes 4194320 | tf_op jit(solution)/shard_map/all_gather | solution.py:125
  48.7 0.0 copy-done
  48.7 6.4 %fusion.10 = f32[512,256]{1,0:T(8,128)} fusion(f32[1,2048,256]{2,1,0:T(8,128)S(1)} %copy-done, f32[1,512,2048]{2,1,0:T(8,128)} %all-gather.17.cloned.1.call-done, f32[512]{0:T(512)S(1)} %fusion.32), kind=kOutput, calls=%fused_computation.13 | convolution fusion | flops 3221356544 | bytes 6817792 | tf_op jit(solution)/shard_map/dot_general | solution.py:44
  55.1 0.0 all-gather.11.cloned.1.call-update
  55.2 49.5 %all-gather.19.cloned.1.call-done = f32[1,2048,512]{2,1,0:T(8,128)} async-done(((f32[1,256,512]{2,1,0:T(8,128)}), f32[1,2048,512]{2,1,0:T(8,128)}) %all-gather.19.cloned.1.call-update) | async-done | bytes 4194320 | tf_op jit(solution)/shard_map/all_gather | solution.py:128
  104.6 6.2 %fusion.15 = f32[256,512]{1,0:T(8,128)S(1)} fusion(f32[1,2048,512]{2,1,0:T(8,128)} %all-gather.19.cloned.1.call-done, f32[1,256,2048]{2,1,0:T(8,128)} %param.15, f32[512]{0:T(512)S(1)} %fusion.33), kind=kOutput, calls=%fused_computation.14 | convolution fusion | flops 3221356544 | bytes 6817792 | tf_op jit(solution)/shard_map/dot_general | solution.py:44
  110.9 0.0 copy-start.2
  110.9 2.5 stack.2
  113.4 0.0 copy-done.2
  113.4 4.7 %all-to-all-start.1 = ((f32[8,256,512]{2,1,0:T(8,128)}), f32[8,256,512]{2,1,0:T(8,128)}, u32[]{:S(2)}, u32[]{:S(2)}) async-start(f32[8,256,512]{2,1,0:T(8,128)} %stack.2), calls=%async_computation.1 | async-start | bytes 8388608 | tf_op jit(solution)/shard_map/all_to_all | solution.py:131
  118.1 0.0 all-gather.13.cloned.1.call-start
  118.2 0.0 copy-done.6
  118.2 0.1 convert_reduce_fusion
  118.3 0.0 copy-start.7
  118.3 143.5 %all-gather.9.cloned.1.call-done = f32[2048,1024]{1,0:T(8,128)} async-done(((f32[64,1024]{1,0:T(8,128)}), f32[2048,1024]{1,0:T(8,128)}) %all-gather.9.cloned.1.call-update) | async-done | bytes 8388624 | tf_op jit(solution)/shard_map/all_gather | solution.py:94
  261.8 0.0 copy-done.4
  261.8 8.2 %fusion.51 = f32[64,1024]{1,0:T(8,128)} fusion(f32[64,2048]{1,0:T(8,128)S(1)} %copy-done.4, f32[2048,1024]{1,0:T(8,128)} %all-gather.9.cloned.1.call-done), kind=kOutput, calls=%fused_computation.69 | convolution fusion | flops 1610612736 | bytes 9175040 | tf_op jit(solution)/shard_map/dot_general | solution.py:44
  270.0 0.0 all-gather.13.cloned.1.call-update
  270.1 0.1 fusion.27
  270.2 0.1 copy.37
  270.3 0.0 copy-done.5
  270.3 0.2 copy.29
  270.5 0.0 copy-done.7
  270.5 0.0 all-to-all-done.1
  270.5 1.5 broadcast_in_dim.16
  272.1 4.8 %all-to-all-start = ((f32[8,256,256]{1,2,0:T(8,128)}), f32[8,256,256]{1,2,0:T(8,128)S(1)}, u32[]{:S(2)}, u32[]{:S(2)}) async-start(f32[8,256,256]{1,2,0:T(8,128)} %broadcast_in_dim.16), calls=%async_computation | async-start | bytes 4194304 | tf_op jit(solution)/shard_map/all_to_all | solution.py:22
  276.9 0.0 all-gather.15.cloned.1.call-start
  276.9 38.4 %all-gather.11.cloned.1.call-done = f32[512,2048]{1,0:T(8,128)} async-done(((f32[512,256]{1,0:T(8,128)}), f32[512,2048]{1,0:T(8,128)}) %all-gather.11.cloned.1.call-update) | async-done | bytes 4194320 | tf_op jit(solution)/shard_map/all_gather | solution.py:135
  315.3 9.4 %convolution_subtract_fusion = f32[512,512]{1,0:T(8,128)S(1)} fusion(f32[512,2048]{1,0:T(8,128)} %all-gather.11.cloned.1.call-done, f32[2048,512]{1,0:T(8,128)} %bitcast.13), kind=kOutput, calls=%fused_computation.11 | convolution fusion | flops 6442713088 | bytes 9437184 | tf_op jit(solution)/shard_map/dot_general | solution.py:44
  324.7 3.6 fusion.20
  328.2 13.9 %all-gather.13.cloned.1.call-done = f32[256,1024]{1,0:T(8,128)} async-done(((f32[64,1024]{1,0:T(8,128)}), f32[256,1024]{1,0:T(8,128)}) %all-gather.13.cloned.1.call-update) | async-done | bytes 1048592 | tf_op jit(solution)/shard_map/all_gather | solution.py:39
  342.2 0.0 all-gather.15.cloned.1.call-update
  342.2 3.1 constant_dynamic-update-slice_fusion
  345.3 1.3 dynamic-update-slice.1
  346.6 1.4 dynamic-update-slice.2
  347.9 4.8 %copy.31 = f32[4,1,131078]{2,1,0:T(1,128)} copy(f32[4,1,131078]{2,0,1:T(4,128)} %bitcast.100) | data formatting | bytes 4194496 | tf_op jit(solution)/shard_map/all_to_all | solution.py:15
  352.8 0.0 all-to-all-done
  352.8 4.5 all-to-all-start.2
  357.3 5.3 %fusion.50 = f32[256,256]{1,0:T(8,128)S(1)} fusion(f32[256,2048]{0,1:T(8,128)S(1)} %bitcast.101, f32[2048,256]{1,0:T(8,128)} %param.22), kind=kOutput, calls=%fused_computation.68 | convolution fusion | flops 1610612736 | bytes 4456448 | tf_op jit(solution)/shard_map/dot_general | solution.py:44
  362.6 0.0 copy-start.3
  362.6 0.1 copy.35
  362.7 18.3 %all-to-all-done.2 = f32[4,1,131078]{2,1,0:T(1,128)} async-done(((f32[4,1,131078]{2,1,0:T(1,128)}), f32[4,1,131078]{2,1,0:T(1,128)}, u32[]{:S(2)}, u32[]{:S(2)}) %all-to-all-start.2) | async-done | bytes 2097280 | tf_op jit(solution)/shard_map/all_to_all | solution.py:15
  381.1 1.5 broadcast_in_dim.20
  382.6 0.0 copy-done.3
  382.6 7.9 %all-to-all-start.3 = ((f32[8,256,256]{1,2,0:T(8,128)}), f32[8,256,256]{1,2,0:T(8,128)}, u32[]{:S(2)}, u32[]{:S(2)}) async-start(f32[8,256,256]{1,2,0:T(8,128)} %broadcast_in_dim.20), calls=%async_computation.3 | async-start | bytes 4194304 | tf_op jit(solution)/shard_map/all_to_all | solution.py:22
  390.5 2.6 copy.53
  393.1 1.5 split.14
  394.6 0.1 split.12
  394.7 3.4 reshape_reshape.7
  398.1 0.1 copy.32
  398.2 4.8 %fusion.8 = f32[4,2,128,4,128]{4,1,3,2,0:T(2,128)S(1)} fusion(f32[4,2,128,4,128]{4,3,2,1,0:T(4,128)S(1)} %reshape_reshape.7, f32[4,2]{1,0:T(4,128)S(1)} %split.13, f32[2]{0:T(128)S(1)} %iota_convert_fusion), kind=kOutput, calls=%fused_computation.9 | convolution fusion | flops 12582928 | bytes 4194344 | tf_op jit(solution)/shard_map/psa,psxjy->paxjy/dot_general | solution.py:84
  403.0 3.2 fusion.6
  406.2 10.6 %all-to-all-done.3 = f32[8,256,256]{1,2,0:T(8,128)} async-done(((f32[8,256,256]{1,2,0:T(8,128)}), f32[8,256,256]{1,2,0:T(8,128)}, u32[]{:S(2)}, u32[]{:S(2)}) %all-to-all-start.3) | async-done | bytes 2097184 | tf_op jit(solution)/shard_map/all_to_all | solution.py:22
  416.8 23.5 %all-gather.15.cloned.1.call-done = f32[2048,1024]{1,0:T(8,128)} async-done(((f32[256,1024]{1,0:T(8,128)}), f32[2048,1024]{1,0:T(8,128)}) %all-gather.15.cloned.1.call-update) | async-done | bytes 8388624 | tf_op jit(solution)/shard_map/all_gather | solution.py:39
  440.2 11.4 %convolution_subtract_fusion.1 = f32[256,1024]{1,0:T(8,128)} fusion(f32[256,2048]{0,1:T(8,128)} %bitcast.29, f32[2048,1024]{1,0:T(8,128)} %all-gather.15.cloned.1.call-done, f32[256,1024]{1,0:T(8,128)} %param.19, f32[32,8,8,128]{3,2,1,0:T(8,128)S(1)} %bitcast.104), kind=kOutput, calls=%fused_computation.12 | convolution fusion | flops 6442975232 | bytes 13631488 | tf_op jit(solution)/shard_map/dot_general | solution.py:44
  451.7 0.0 copy-done.1
  (16 shorter events, 0.1 us)
Async XLA Ops:
  7.2 41.5 %copy-start = (f32[1,2048,256]{2,1,0:T(8,128)S(1)}, f32[1,2048,256]{2,1,0:T(8,128)}, u32[]{:S(2)}) copy-start(f32[1,2048,256]{2,1,0:T(8,128)} %param.14) | copy-start | bytes 6291460
  7.2 41.5 %all-gather.17.cloned.1.call-start = ((), (), s32[]{:S(2)}) async-start(), calls=%async_computation.8 | async-start | bytes 4718592 | tf_op jit(solution)/shard_map/all_gather | solution.py:125
  7.9 96.7 %all-gather.19.cloned.1.call-start = ((), (), s32[]{:S(2)}) async-start(), calls=%async_computation.9 | async-start | bytes 4718592 | tf_op jit(solution)/shard_map/all_gather | solution.py:128
  8.7 253.2 %all-gather.9.cloned.1.call-start = ((), (), s32[]{:S(2)}) async-start(), calls=%async_computation.4 | async-start | bytes 8650752 | tf_op jit(solution)/shard_map/all_gather | solution.py:94
  9.4 305.9 %all-gather.11.cloned.1.call-start = ((), (), s32[]{:S(2)}) async-start(), calls=%async_computation.5 | async-start | bytes 4718592 | tf_op jit(solution)/shard_map/all_gather | solution.py:135
  110.9 2.5 copy-start.2
  113.4 4.8 %copy-start.6 = (s32[1,4]{1,0:T(1,128)S(1)}, s32[1,4]{1,0:T(1,128)}, u32[]{:S(2)}) copy-start(s32[1,4]{1,0:T(1,128)} %param.17) | copy-start | bytes 52
  113.4 148.5 %copy-start.4 = (f32[64,2048]{1,0:T(8,128)S(1)}, f32[64,2048]{1,0:T(8,128)}, u32[]{:S(2)}) copy-start(f32[64,2048]{1,0:T(8,128)} %param.23) | copy-start | bytes 1572868
  113.4 157.2 %all-to-all-start.1 = ((f32[8,256,512]{2,1,0:T(8,128)}), f32[8,256,512]{2,1,0:T(8,128)}, u32[]{:S(2)}, u32[]{:S(2)}) async-start(f32[8,256,512]{2,1,0:T(8,128)} %stack.2), calls=%async_computation.1 | async-start | bytes 8388608 | tf_op jit(solution)/shard_map/all_to_all | solution.py:131
  118.1 224.1 %all-gather.13.cloned.1.call-start = ((), (), s32[]{:S(2)}) async-start(), calls=%async_computation.6 | async-start | bytes 1310720 | tf_op jit(solution)/shard_map/all_gather | solution.py:39
  118.3 152.0 %copy-start.5 = (f32[256,256]{1,0:T(8,128)S(1)}, f32[256,256]{1,0:T(8,128)}, u32[]{:S(2)}) copy-start(f32[256,256]{1,0:T(8,128)} %param.20) | copy-start | bytes 786436
  118.3 152.2 %copy-start.7 = (s32[1,4]{1,0:T(1,128)S(1)}, s32[1,4]{1,0:T(1,128)}, u32[]{:S(2)}) copy-start(s32[1,4]{1,0:T(1,128)} %param.18) | copy-start | bytes 52
  272.1 80.7 %all-to-all-start = ((f32[8,256,256]{1,2,0:T(8,128)}), f32[8,256,256]{1,2,0:T(8,128)S(1)}, u32[]{:S(2)}, u32[]{:S(2)}) async-start(f32[8,256,256]{1,2,0:T(8,128)} %broadcast_in_dim.16), calls=%async_computation | async-start | bytes 4194304 | tf_op jit(solution)/shard_map/all_to_all | solution.py:22
  276.9 163.3 %all-gather.15.cloned.1.call-start = ((), (), s32[]{:S(2)}) async-start(), calls=%async_computation.7 | async-start | bytes 9437184 | tf_op jit(solution)/shard_map/all_gather | solution.py:39
  352.8 28.3 %all-to-all-start.2 = ((f32[4,1,131078]{2,1,0:T(1,128)}), f32[4,1,131078]{2,1,0:T(1,128)}, u32[]{:S(2)}, u32[]{:S(2)}) async-start(f32[4,1,131078]{2,1,0:T(1,128)} %copy.31), calls=%async_computation.2 | async-start | bytes 4198400 | tf_op jit(solution)/shard_map/all_to_all | solution.py:15
  362.6 20.0 %copy-start.3 = (f32[256,256]{1,0:T(8,128)}, f32[256,256]{1,0:T(8,128)S(1)}, u32[]{:S(2)}) copy-start(f32[256,256]{1,0:T(8,128)S(1)} %fusion.50) | copy-start | bytes 786436
  382.6 34.2 %all-to-all-start.3 = ((f32[8,256,256]{1,2,0:T(8,128)}), f32[8,256,256]{1,2,0:T(8,128)}, u32[]{:S(2)}, u32[]{:S(2)}) async-start(f32[8,256,256]{1,2,0:T(8,128)} %broadcast_in_dim.20), calls=%async_computation.3 | async-start | bytes 4194304 | tf_op jit(solution)/shard_map/all_to_all | solution.py:22
  440.2 11.4 %copy-start.1 = (f32[1,2048,256]{2,1,0:T(8,128)S(1)}, f32[1,2048,256]{2,1,0:T(8,128)}, u32[]{:S(2)}) copy-start(f32[1,2048,256]{2,1,0:T(8,128)} %param.14) | copy-start | bytes 6291460
Sparse Core Ops, SparseCore 0:
  9.8 38.8 all-gather.16
  50.5 54.1 all-gather.18
  107.2 154.5 all-gather.8
  264.1 51.1 all-gather.10
  317.5 24.6 all-gather.12
  343.8 96.3 all-gather.14
